TPU v7x, 32 devices: a whole 2x2x4 slice. The times are simulated.
32 devices in a mesh: tile: 8 (over z, x), cls: 4 (over y, core).
Axes of the slice: x: 2, y: 2, z: 4, core: 2. Of those that a mesh axis runs over, the one named last changes fastest.
Arguments:
- concentration: float32 [64, 4, 16384], P('cls', None, 'tile'), may hold values from 0.05 to 2
- velocity: float32 [2, 4, 16384], P(None, None, 'tile'), may hold values from -0.3 to 0.3
- land_mask: int32 [16384], P('tile'), may hold values 0 or 1
- settling: float32 [64], P('cls'), may hold values from 0.01 to 0.3
- breakage_rate: float32 [64], replicated, may hold values from 0.02 to 0.3
- kernel_levels: int32 [64, 64], replicated, may hold values from 100 to 1000, as said below
- pair_target: int32 [64, 64], replicated, may hold values from 0 to 63, as said below
- fragment_weights: int32 [64, 64], replicated, may hold values from 1 to 16
Outputs:
- flocs: float32 [64, 4, 16384], P('cls', None, 'tile')
Inputs may be any that keep to these rules, and one draw needn't show every extreme that they name: `kernel_levels`: symmetric. `pair_target`: symmetric, and entry [i, j] is at least the larger of i and j.
All inputs are finite; a program needn't handle non-finite values. No bound on the sum of `land_mask` on one device may be relied on, other than what follows from the above.
Results may differ from a plain program's by a relative error of at most 0.0001.
Values sent between devices are 32-bit elements; how exact they have to be, the bound alone decides.
A program may use at most 64 MiB of HBM per device.

v0:
```python
import jax
import jax.numpy as jnp
from jax import lax
from jax.sharding import PartitionSpec as P

CY = 512
CX = 4


kernel_scale = 1e-05
temp_floats = 2097152


def passed_along(x, axis, by):
    length = lax.axis_size(axis)
    pairs = [(i, i + by) for i in range(length) if 0 <= i + by < length]
    return lax.ppermute(x, axis, pairs)


def face_flux(low, high, group, part):
    speed = 0.5 * (low[group + part] + high[group + part]) * low[group + 2] * high[group + 2]
    return jnp.maximum(speed, 0.0) * low[:group] + jnp.minimum(speed, 0.0) * high[:group]


def make_tables(start, count, kernel_levels, pair_target, fragment_weights, breakage_rate):
    total = kernel_levels.shape[0]
    levels = kernel_levels.astype(jnp.float32) * kernel_scale
    rank = jnp.arange(total, dtype=jnp.int32)
    mine = start + jnp.arange(count, dtype=jnp.int32)
    hit = pair_target[None, :, :] == mine[:, None, None]
    birth = jnp.where(hit, 0.5 * levels[None, :, :], 0.0)
    pairs = jnp.transpose(birth, (1, 0, 2)).reshape(total * count, total)
    lower = jnp.where(rank[:, None] <= rank[None, :], fragment_weights.astype(jnp.float32), 0.0)
    frag = lower / jnp.sum(lower, axis=0, keepdims=True)
    kernel_rows = lax.dynamic_slice_in_dim(levels, start, count, 0)
    frag_rows = lax.dynamic_slice_in_dim(frag, start, count, 0)
    rate_rows = lax.dynamic_slice_in_dim(breakage_rate, start, count, 0)
    return (pairs, kernel_rows, frag_rows, rate_rows)


def react(own, whole, tables, breakage_rate):
    pairs, kernel_rows, frag_rows, rate_rows = tables
    count, width = own.shape
    total = whole.shape[0]
    block = max(1, min(width, temp_floats // (total * count)))
    while width % block != 0:
        block = block - 1
    steps_count = width // block

    def add_block(index, gain):
        offset = index * block
        cols = lax.dynamic_slice_in_dim(whole, offset, block, 1)
        made = jnp.dot(
            pairs, cols, precision=lax.Precision.HIGHEST, preferred_element_type=jnp.float32
        )
        part_gain = jnp.sum(made.reshape(total, count, block) * cols[:, None, :], axis=0)
        return lax.dynamic_update_slice_in_dim(gain, part_gain, offset, 1)

    gain = lax.fori_loop(0, steps_count, add_block, jnp.zeros((count, width), jnp.float32))
    loss = own * jnp.dot(
        kernel_rows, whole, precision=lax.Precision.HIGHEST, preferred_element_type=jnp.float32
    )
    broken = (
        jnp.dot(
            frag_rows,
            breakage_rate[:, None] * whole,
            precision=lax.Precision.HIGHEST,
            preferred_element_type=jnp.float32,
        )
        - rate_rows[:, None] * own
    )
    return own + gain - loss + broken


def body(
    concentration,
    velocity,
    land_mask,
    settling,
    breakage_rate,
    kernel_levels,
    pair_target,
    fragment_weights,
):
    group, layers, columns = concentration.shape
    field = concentration.reshape(group, layers, CX, CY)
    water = land_mask.astype(jnp.float32).reshape(1, 1, CX, CY)
    stacked = jnp.concatenate(
        [field, velocity.reshape(2, layers, CX, CY), jnp.broadcast_to(water, (1, layers, CX, CY))],
        0,
    )
    west = passed_along(stacked[:, :, CX - 1 :, :], "tile", 1)
    east = passed_along(stacked[:, :, :1, :], "tile", -1)
    along_x = jnp.concatenate([west, stacked, east], 2)
    along_y = jnp.pad(stacked, ((0, 0), (0, 0), (0, 0), (1, 1)))
    flux_x = face_flux(along_x[:, :, :-1], along_x[:, :, 1:], group, 0)
    flux_y = face_flux(along_y[:, :, :, :-1], along_y[:, :, :, 1:], group, 1)
    moved = (
        field
        - (flux_x[:, :, 1:] - flux_x[:, :, :-1])
        - (flux_y[:, :, :, 1:] - flux_y[:, :, :, :-1])
    )
    sink = settling[:, None, None, None] * field
    moved = moved - sink + jnp.pad(sink[:, :-1], ((0, 0), (1, 0), (0, 0), (0, 0)))
    current = moved.reshape(group, layers * columns)
    start = lax.axis_index("cls") * group
    tables = make_tables(start, group, kernel_levels, pair_target, fragment_weights, breakage_rate)
    for sub in range(2):
        whole = lax.all_gather(current, "cls", axis=0, tiled=True)
        current = react(current, whole, tables, breakage_rate)
    return current.reshape(group, layers, columns)


def solution(mesh):
    return jax.shard_map(
        body,
        mesh=mesh,
        in_specs=(
            P("cls", None, "tile"),
            P(None, None, "tile"),
            P("tile"),
            P("cls"),
            P(),
            P(),
            P(),
            P(),
        ),
        out_specs=P("cls", None, "tile"),
        check_vma=False,
    )
```

profile of v0, /device:TPU:9, one launch (start us, length us, event | category | flops | bytes accessed | tf_op | source)
XLA Modules:
  0.0 163.0 jit_solution(15692153921223102179)
XLA Ops:
  6.5 1.5 reshape.47
  8.0 0.9 reshape.48
  8.9 0.7 convert_element_type.13
  9.9 0.2 fusion.36
  10.1 3.1 %collective-permute-start = (f32[19,4,1,512]{3,2,1,0:T(1,128)S(1)}, f32[19,4,1,512]{3,2,1,0:T(1,128)S(1)}, u32[]{:S(2)}, u32[]{:S(2)}) collective-permute-start(f32[19,4,1,512]{3,2,1,0:T(1,128)S(1)} %get-tuple-element.227), channel_id=1, source_target_pairs={{0,4},{4,8},{8,12},{12,16},{16,20},{20,24},{24,28},{1,5},{5,9},{9,... | collective-permute-start | bytes 466952 | tf_op jit(solution)/shard_map/ppermute | solution.py:17
  13.2 3.1 %collective-permute-start.1 = (f32[19,4,1,512]{3,2,1,0:T(1,128)S(1)}, f32[19,4,1,512]{3,2,1,0:T(1,128)S(1)}, u32[]{:S(2)}, u32[]{:S(2)}) collective-permute-start(f32[19,4,1,512]{3,2,1,0:T(1,128)S(1)} %get-tuple-element.228), channel_id=1, source_target_pairs={{4,0},{8,4},{12,8},{16,12},{20,16},{24,20},{28,24},{5,1},{9,5},{13... | collective-permute-start | bytes 466952 | tf_op jit(solution)/shard_map/ppermute | solution.py:17
  16.6 0.4 fusion.16
  17.1 0.7 collective-permute-done
  17.8 4.2 %collective-permute-done.1 = f32[19,4,1,512]{3,2,1,0:T(1,128)S(1)} collective-permute-done((f32[19,4,1,512]{3,2,1,0:T(1,128)S(1)}, f32[19,4,1,512]{3,2,1,0:T(1,128)S(1)}, u32[]{:S(2)}, u32[]{:S(2)}) %collective-permute-start.1) | collective-permute-done | bytes 155680 | tf_op jit(solution)/shard_map/ppermute | solution.py:17
  22.1 0.5 fusion.11
  22.6 0.6 fusion.20
  23.2 1.2 reshape.49
  24.4 0.2 all-gather.5.cloned.1.call-start
  24.8 22.9 %all-gather.3.cloned.1.call-done = f32[64,8192]{1,0:T(8,128)} async-done(((f32[16,8192]{1,0:T(8,128)}), f32[64,8192]{1,0:T(8,128)}) %all-gather.3.cloned.1.call-update) | async-done | bytes 2097168 | tf_op jit(solution)/shard_map/all_gather | solution.py:109
  47.8 37.6 %while.28 = (s32[]{:T(128)}, f32[16,8192]{1,0:T(8,128)S(1)}, f32[64,8192]{1,0:T(8,128)}, s32[64,64]{1,0:T(8,128)S(1)}, s32[1024]{0:T(1024)S(1)}, /*index=5*/f32[...) while((s32[]{:T(128)}, f32[16,8192]{1,0:T(8,128)S(1)}, f32[64,8192]{1,0:T(8,128)}, ...), condition=%wide.region_2.3_spmd.clone, body=%wide.region_0.2_spmd.clone.sunk | while | flops 1614905344 | bytes 19828892 | solution.py:59
  47.8 1.1 constant_dynamic-slice_fusion.4
  49.0 0.2 bitcast_select_fusion.4
  49.2 6.7 %fusion.53 = f32[2048,1024]{0,1:T(8,128)S(1)} fusion(f32[64,2048]{1,0:T(8,128)S(1)} %constant_dynamic-slice_fusion.4, f32[1024,64]{1,0:T(8,128)S(1)} %bitcast_select_fusion.4), kind=kOutput, calls=%fused_computation.77.clone.1 | convolution fusion | flops 1610612736 | bytes 9175040 | tf_op jit(solution)/shard_map/while/body/eval_jaxpr/dot_general | solution.py:53
  55.9 1.4 multiply_reduce_fusion.4
  57.3 1.1 constant_dynamic-slice_fusion.4
  58.4 0.2 bitcast_select_fusion.4
  58.6 6.7 %fusion.53 = f32[2048,1024]{0,1:T(8,128)S(1)} fusion(f32[64,2048]{1,0:T(8,128)S(1)} %constant_dynamic-slice_fusion.4, f32[1024,64]{1,0:T(8,128)S(1)} %bitcast_select_fusion.4), kind=kOutput, calls=%fused_computation.77.clone.1 | convolution fusion | flops 1610612736 | bytes 9175040 | tf_op jit(solution)/shard_map/while/body/eval_jaxpr/dot_general | solution.py:53
  65.2 1.4 multiply_reduce_fusion.4
  66.7 1.1 constant_dynamic-slice_fusion.4
  68.0 6.7 %fusion.53 = f32[2048,1024]{0,1:T(8,128)S(1)} fusion(f32[64,2048]{1,0:T(8,128)S(1)} %constant_dynamic-slice_fusion.4, f32[1024,64]{1,0:T(8,128)S(1)} %bitcast_select_fusion.4), kind=kOutput, calls=%fused_computation.77.clone.1 | convolution fusion | flops 1610612736 | bytes 9175040 | tf_op jit(solution)/shard_map/while/body/eval_jaxpr/dot_general | solution.py:53
  74.6 1.4 multiply_reduce_fusion.4
  76.0 1.1 constant_dynamic-slice_fusion.4
  77.3 6.7 %fusion.53 = f32[2048,1024]{0,1:T(8,128)S(1)} fusion(f32[64,2048]{1,0:T(8,128)S(1)} %constant_dynamic-slice_fusion.4, f32[1024,64]{1,0:T(8,128)S(1)} %bitcast_select_fusion.4), kind=kOutput, calls=%fused_computation.77.clone.1 | convolution fusion | flops 1610612736 | bytes 9175040 | tf_op jit(solution)/shard_map/while/body/eval_jaxpr/dot_general | solution.py:53
  84.0 1.4 multiply_reduce_fusion.4
  85.4 2.8 %fusion.7 = f32[16,8192]{1,0:T(8,128)S(1)} fusion(f32[16,8192]{1,0:T(8,128)S(1)} %copy-done.3, f32[64,8192]{1,0:T(8,128)} %get-tuple-element.368, f32[16,8192]{1,0:T(8,128)S(1)} %get-tuple-element.163, f32[64,64]{1,0:T(8,128)S(1)} %convert_element_type.14, s32[]{:T(128)S(6)} %select_n.32), kind=kOutput, calls=%fused_computation.19 | convolution fusion | flops 101057536 | bytes 3678212 | tf_op jit(solution)/shard_map/dot_general | solution.py:60
  88.3 2.0 %fusion.6 = f32[16,8192]{1,0:T(8,128)} fusion(f32[16,8192]{1,0:T(8,128)S(1)} %fusion.7, f32[64,8192]{1,0:T(8,128)S(1)} %copy-done, f32[64]{0:T(128)S(1)} %copy-done.7, f32[16,8192]{1,0:T(8,128)S(1)} %copy-done.3, f32[16]{0:T(128)S(1)} %dynamic_slice.25, f32[64,64]{1,0:T(8,128)S(1)} %get-tuple-element.230, s32[]{:T(128)S(6)} %select_n.32, ...), kind=kOutput, calls=%fused_computation.17 | convolution fusion | flops 101581824 | bytes 3679748 | tf_op jit(solution)/shard_map/dot_general | solution.py:64
  90.4 22.7 %all-gather.5.cloned.1.call-done = f32[64,8192]{1,0:T(8,128)} async-done(((f32[16,8192]{1,0:T(8,128)}), f32[64,8192]{1,0:T(8,128)}) %all-gather.5.cloned.1.call-update) | async-done | bytes 2097168 | tf_op jit(solution)/shard_map/all_gather | solution.py:109
  113.1 37.8 %while.29 = (s32[]{:T(128)}, f32[16,8192]{1,0:T(8,128)S(1)}, f32[64,8192]{1,0:T(8,128)}, s32[64,64]{1,0:T(8,128)S(1)}, s32[1024]{0:T(1024)S(1)}, /*index=5*/f32[...) while((s32[]{:T(128)}, f32[16,8192]{1,0:T(8,128)S(1)}, f32[64,8192]{1,0:T(8,128)}, ...), condition=%wide.region_6.7_spmd.clone, body=%wide.region_4.6_spmd.clone.sunk | while | flops 1614905344 | bytes 19828892 | solution.py:59
  113.4 1.1 constant_dynamic-slice_fusion.5
  114.7 6.7 %fusion.56 = f32[2048,1024]{0,1:T(8,128)S(1)} fusion(f32[64,2048]{1,0:T(8,128)S(1)} %constant_dynamic-slice_fusion.5, f32[1024,64]{1,0:T(8,128)S(1)} %bitcast_select_fusion.5), kind=kOutput, calls=%fused_computation.78.clone.1 | convolution fusion | flops 1610612736 | bytes 9175040 | tf_op jit(solution)/shard_map/while/body/eval_jaxpr/dot_general | solution.py:53
  121.3 1.4 multiply_reduce_fusion.5
  122.8 1.1 constant_dynamic-slice_fusion.5
  124.1 6.7 %fusion.56 = f32[2048,1024]{0,1:T(8,128)S(1)} fusion(f32[64,2048]{1,0:T(8,128)S(1)} %constant_dynamic-slice_fusion.5, f32[1024,64]{1,0:T(8,128)S(1)} %bitcast_select_fusion.5), kind=kOutput, calls=%fused_computation.78.clone.1 | convolution fusion | flops 1610612736 | bytes 9175040 | tf_op jit(solution)/shard_map/while/body/eval_jaxpr/dot_general | solution.py:53
  130.7 1.4 multiply_reduce_fusion.5
  132.2 1.1 constant_dynamic-slice_fusion.5
  133.4 6.7 %fusion.56 = f32[2048,1024]{0,1:T(8,128)S(1)} fusion(f32[64,2048]{1,0:T(8,128)S(1)} %constant_dynamic-slice_fusion.5, f32[1024,64]{1,0:T(8,128)S(1)} %bitcast_select_fusion.5), kind=kOutput, calls=%fused_computation.78.clone.1 | convolution fusion | flops 1610612736 | bytes 9175040 | tf_op jit(solution)/shard_map/while/body/eval_jaxpr/dot_general | solution.py:53
  140.1 1.4 multiply_reduce_fusion.5
  141.5 1.1 constant_dynamic-slice_fusion.5
  142.8 6.7 %fusion.56 = f32[2048,1024]{0,1:T(8,128)S(1)} fusion(f32[64,2048]{1,0:T(8,128)S(1)} %constant_dynamic-slice_fusion.5, f32[1024,64]{1,0:T(8,128)S(1)} %bitcast_select_fusion.5), kind=kOutput, calls=%fused_computation.78.clone.1 | convolution fusion | flops 1610612736 | bytes 9175040 | tf_op jit(solution)/shard_map/while/body/eval_jaxpr/dot_general | solution.py:53
  149.5 1.4 multiply_reduce_fusion.5
  150.9 2.8 %fusion.5 = f32[16,8192]{1,0:T(8,128)S(1)} fusion(f32[16,8192]{1,0:T(8,128)S(1)} %copy-done.2, f32[64,8192]{1,0:T(8,128)} %get-tuple-element.370, f32[16,8192]{1,0:T(8,128)S(1)} %get-tuple-element.164, f32[64,64]{1,0:T(8,128)S(1)} %convert_element_type.14, s32[]{:T(128)S(6)} %select_n.32), kind=kOutput, calls=%fused_computation.15 | convolution fusion | flops 101057536 | bytes 3678212 | tf_op jit(solution)/shard_map/dot_general | solution.py:60
  153.8 1.2 fusion.4
  155.0 1.1 reshape.50
  (53 shorter events, 2.3 us)
Async XLA Ops:
  6.5 9.9 %copy-start.8 = (f32[16]{0:T(128)S(1)}, f32[16]{0:T(128)}, u32[]{:S(2)}) copy-start(f32[16]{0:T(128)} %param.15) | copy-start | bytes 196
  6.5 41.2 %all-gather.3.cloned.1.call-start = ((), (), s32[]{:S(2)}) async-start(), calls=%async_computation | async-start | bytes 2621440 | tf_op jit(solution)/shard_map/all_gather | solution.py:109
  10.1 7.7 %collective-permute-start = (f32[19,4,1,512]{3,2,1,0:T(1,128)S(1)}, f32[19,4,1,512]{3,2,1,0:T(1,128)S(1)}, u32[]{:S(2)}, u32[]{:S(2)}) collective-permute-start(f32[19,4,1,512]{3,2,1,0:T(1,128)S(1)} %get-tuple-element.227), channel_id=1, source_target_pairs={{0,4},{4,8},{8,12},{12,16},{16,20},{20,24},{24,28},{1,5},{5,9},{9,... | collective-permute-start | bytes 466952 | tf_op jit(solution)/shard_map/ppermute | solution.py:17
  13.2 8.7 %collective-permute-start.1 = (f32[19,4,1,512]{3,2,1,0:T(1,128)S(1)}, f32[19,4,1,512]{3,2,1,0:T(1,128)S(1)}, u32[]{:S(2)}, u32[]{:S(2)}) collective-permute-start(f32[19,4,1,512]{3,2,1,0:T(1,128)S(1)} %get-tuple-element.228), channel_id=1, source_target_pairs={{4,0},{8,4},{12,8},{16,12},{20,16},{24,20},{28,24},{5,1},{9,5},{13... | collective-permute-start | bytes 466952 | tf_op jit(solution)/shard_map/ppermute | solution.py:17
  22.5 2.2 %copy-start.5 = (s32[64,64]{1,0:T(8,128)S(1)}, s32[64,64]{1,0:T(8,128)}, u32[]{:S(2)}) copy-start(s32[64,64]{1,0:T(8,128)} %param.17) | copy-start | bytes 49156
  22.5 2.2 %copy-start.7 = (f32[64]{0:T(128)S(1)}, f32[64]{0:T(128)}, u32[]{:S(2)}) copy-start(f32[64]{0:T(128)} %param.16) | copy-start | bytes 772
  22.5 2.3 %copy-start.6 = (s32[64,64]{1,0:T(8,128)S(1)}, s32[64,64]{1,0:T(8,128)}, u32[]{:S(2)}) copy-start(s32[64,64]{1,0:T(8,128)} %param.19) | copy-start | bytes 49156
  22.5 25.2 %copy-start.4 = (s32[64,64]{1,0:T(8,128)S(1)}, s32[64,64]{1,0:T(8,128)}, u32[]{:S(2)}) copy-start(s32[64,64]{1,0:T(8,128)} %param.18) | copy-start | bytes 49156
  24.4 88.7 %all-gather.5.cloned.1.call-start = ((), (), s32[]{:S(2)}) async-start(), calls=%async_computation.1 | async-start | bytes 2621440 | tf_op jit(solution)/shard_map/all_gather | solution.py:109
  47.8 37.6 %copy-start.3 = (f32[16,8192]{1,0:T(8,128)S(1)}, f32[16,8192]{1,0:T(8,128)}, u32[]{:S(2)}) copy-start(f32[16,8192]{1,0:T(8,128)} %reshape.49) | copy-start | bytes 1572868
  85.4 2.9 %copy-start = (f32[64,8192]{1,0:T(8,128)S(1)}, f32[64,8192]{1,0:T(8,128)}, u32[]{:S(2)}) copy-start(f32[64,8192]{1,0:T(8,128)} %get-tuple-element.368) | copy-start | bytes 6291460
  113.1 37.8 %copy-start.2 = (f32[16,8192]{1,0:T(8,128)S(1)}, f32[16,8192]{1,0:T(8,128)}, u32[]{:S(2)}) copy-start(f32[16,8192]{1,0:T(8,128)} %fusion.6) | copy-start | bytes 1572868
  150.9 2.9 %copy-start.1 = (f32[64,8192]{1,0:T(8,128)S(1)}, f32[64,8192]{1,0:T(8,128)}, u32[]{:S(2)}) copy-start(f32[64,8192]{1,0:T(8,128)} %get-tuple-element.370) | copy-start | bytes 6291460
Sparse Core Ops, SparseCore 0:
  24.5 23.2 all-gather.2
  90.5 22.5 all-gather.4
where the time goes:
time: 165 us; the launch traced here: 163 us
  matrix products  62.4 us (38%)
  waiting for transfers between devices  50.6 us (31%)
  other arithmetic  15.3 us (9%)
  local copies, waits for them, and re-layouts  14.1 us (9%)
  between operations  13.7 us (8%)
  starting transfers between devices  6.41 us (4%)
    dot_general x8, matrix products, add_block(): jnp.dot(pairs, cols, precision=lax.Precision.HIGHEST, preferred_element_t...  53.4 us
    all_gather x2, waiting for transfers between devices, body(): whole = lax.all_gather(current, 'cls', axis=0, tiled=True)  45.6 us
    reduce_sum x8, other arithmetic, add_block(): jnp.sum(made.reshape(total, count, block) * cols[:, None, :], axis=0)  10.9 us
    dynamic_slice x8, local copies, waits for them, and re-layouts, add_block(): cols = lax.dynamic_slice_in_dim(whole, offset, block, 1)  8.71 us
    ppermute x2, starting transfers between devices, passed_along(): return lax.ppermute(x, axis, pairs)  6.18 us
    dot_general x2, matrix products, react(): jnp.dot(kernel_rows, whole, precision=lax.Precision.HIGHEST, preferred_el...  5.69 us
    ppermute x2, waiting for transfers between devices, passed_along(): return lax.ppermute(x, axis, pairs)  4.9 us
  transfers between devices with their start and end apart: 4, of which 4 were waited for; matrix products, arithmetic and copies ran while one was open for 1% of the time, Pallas kernels for 0%

commit v1 on v0

v1 whole, which is shorter than its diff:
```python
import jax
import jax.numpy as jnp
from jax import lax
from jax.experimental import pallas as pl
from jax.experimental.pallas import tpu as pltpu
from jax.sharding import PartitionSpec as P

CY = 512
CX = 4
half_scale = 0.5e-05
STEP = 16


def passed_along(x, axis, by):
    length = lax.axis_size(axis)
    pairs = [(i, i + by) for i in range(length) if 0 <= i + by < length]
    return lax.ppermute(x, axis, pairs)


def face_flux(low, high, group, part):
    speed = 0.5 * (low[group + part] + high[group + part]) * low[group + 2] * high[group + 2]
    return jnp.maximum(speed, 0.0) * low[:group] + jnp.minimum(speed, 0.0) * high[:group]


def split_pair(value, lane, total):
    high = value.astype(jnp.bfloat16).astype(jnp.float32)
    return jnp.where(lane < total, high, value - high).astype(jnp.bfloat16)


def quad_rows(total):
    return sum(STEP * (total - first) for first in range(0, total, STEP))


def build_tables(levels_ref, target_ref, weights_ref, rate_ref, quad_ref, lin_ref):
    total = levels_ref.shape[0]
    wide = 2 * total
    levels = levels_ref[...].astype(jnp.float32)
    levels = jnp.concatenate([levels, levels], 1)
    target = target_ref[...]
    target = jnp.concatenate([target, target], 1)
    row = lax.broadcasted_iota(jnp.int32, (total, wide), 0)
    lane = lax.broadcasted_iota(jnp.int32, (total, wide), 1)
    col = jnp.where(lane < total, lane, lane - total)
    twice = 2.0 * levels
    birth = jnp.where(col < row, twice, jnp.where(col == row, levels, 0.0))
    offset = 0
    for first in range(0, total, STEP):
        count = total - first
        rank = row[first:]
        for i in range(first, first + STEP):
            value = jnp.where(target[i : i + 1] == rank, birth[i : i + 1], 0.0)
            value = value - jnp.where(rank == i, twice[i : i + 1], 0.0)
            packed = split_pair(value, lane[first:], total)
            quad_ref[offset : offset + count, :wide] = packed
            quad_ref[offset : offset + count, wide:] = packed
            offset += count
    weights = weights_ref[...].astype(jnp.float32)
    weights = jnp.concatenate([weights, weights], 1)
    rate = rate_ref[...]
    rate = jnp.concatenate([rate, rate], 1)
    lower = jnp.where(row <= col, weights, 0.0)
    frag = lower / jnp.sum(lower, axis=0, keepdims=True)
    value = frag * rate - jnp.where(row == col, rate, 0.0)
    packed = split_pair(value, lane, total)
    lin_ref[:, :wide] = packed
    lin_ref[:, wide:] = packed


def react(now, quad_ref, lin_ref):
    total = now.shape[0]
    high = now.astype(jnp.bfloat16)
    low = (now - high.astype(jnp.float32)).astype(jnp.bfloat16)
    stack = jnp.concatenate([high, high, low, low], 0)
    lin = jnp.dot(lin_ref[...], stack, preferred_element_type=jnp.float32)
    gain = None
    offset = 0
    for first in range(0, total, STEP):
        count = total - first
        made = jnp.dot(
            quad_ref[offset : offset + STEP * count, :], stack, preferred_element_type=jnp.float32
        )
        part = made[:count] * now[first : first + 1]
        for r in range(1, STEP):
            part = part + made[r * count : (r + 1) * count] * now[first + r : first + r + 1]
        gain = part if gain is None else jnp.concatenate([gain[:first], gain[first:] + part], 0)
        offset += STEP * count
    return now + gain * half_scale + lin


def react_kernel(chunk, levels_ref, target_ref, weights_ref, rate_ref, whole_ref, out_ref, quad_ref, lin_ref):
    build_tables(levels_ref, target_ref, weights_ref, rate_ref, quad_ref, lin_ref)

    def step(index, carry):
        at = pl.ds(pl.multiple_of(index * chunk, chunk), chunk)
        now = react(whole_ref[:, at], quad_ref, lin_ref)
        out_ref[:, at] = react(now, quad_ref, lin_ref)
        return carry

    lax.fori_loop(0, whole_ref.shape[1] // chunk, step, 0)


def react_all(whole, breakage_rate, kernel_levels, pair_target, fragment_weights):
    total, width = whole.shape
    vmem = pl.BlockSpec(memory_space=pltpu.VMEM)
    import functools

    return pl.pallas_call(
        functools.partial(react_kernel, 256),
        out_shape=jax.ShapeDtypeStruct(whole.shape, jnp.float32),
        in_specs=[vmem] * 5,
        out_specs=vmem,
        scratch_shapes=[
            pltpu.VMEM((quad_rows(total), 4 * total), jnp.bfloat16),
            pltpu.VMEM((total, 4 * total), jnp.bfloat16),
        ],
    )(kernel_levels, pair_target, fragment_weights, breakage_rate.reshape(1, total), whole)


def body(
    concentration,
    velocity,
    land_mask,
    settling,
    breakage_rate,
    kernel_levels,
    pair_target,
    fragment_weights,
):
    group, layers, columns = concentration.shape
    field = concentration.reshape(group, layers, CX, CY)
    water = land_mask.astype(jnp.float32).reshape(1, 1, CX, CY)
    stacked = jnp.concatenate(
        [field, velocity.reshape(2, layers, CX, CY), jnp.broadcast_to(water, (1, layers, CX, CY))],
        0,
    )
    west = passed_along(stacked[:, :, CX - 1 :, :], "tile", 1)
    east = passed_along(stacked[:, :, :1, :], "tile", -1)
    along_x = jnp.concatenate([west, stacked, east], 2)
    along_y = jnp.pad(stacked, ((0, 0), (0, 0), (0, 0), (1, 1)))
    flux_x = face_flux(along_x[:, :, :-1], along_x[:, :, 1:], group, 0)
    flux_y = face_flux(along_y[:, :, :, :-1], along_y[:, :, :, 1:], group, 1)
    moved = (
        field
        - (flux_x[:, :, 1:] - flux_x[:, :, :-1])
        - (flux_y[:, :, :, 1:] - flux_y[:, :, :, :-1])
    )
    sink = settling[:, None, None, None] * field
    moved = moved - sink + jnp.pad(sink[:, :-1], ((0, 0), (1, 0), (0, 0), (0, 0)))
    current = moved.reshape(group, layers, columns)
    whole = lax.all_to_all(current, "cls", 1, 0, tiled=True)
    shape = whole.shape
    done = react_all(
        whole.reshape(shape[0], -1), breakage_rate, kernel_levels, pair_target, fragment_weights
    )
    return lax.all_to_all(done.reshape(shape), "cls", 0, 1, tiled=True)


def solution(mesh):
    return jax.shard_map(
        body,
        mesh=mesh,
        in_specs=(
            P("cls", None, "tile"),
            P(None, None, "tile"),
            P("tile"),
            P("cls"),
            P(),
            P(),
            P(),
            P(),
        ),
        out_specs=P("cls", None, "tile"),
        check_vma=False,
    )
```

time: 165 us -> 54.7 us (0.33)
  the two profiles are of different devices: /device:TPU:9 before, /device:TPU:0 now
where the time goes in v1:
time: 54.7 us; the launch traced here: 54.3 us
  blocking collectives  23.1 us (42%)
  Pallas kernels  11.1 us (20%)
  local copies, waits for them, and re-layouts  7.89 us (14%)
  starting transfers between devices  6.17 us (11%)
  waiting for transfers between devices  3.92 us (7%)
  other arithmetic  2.03 us (4%)
    all_to_all x1, blocking collectives, body(): whole = lax.all_to_all(current, 'cls', 1, 0, tiled=True)  11.9 us
    all_to_all x1, blocking collectives, body(): return lax.all_to_all(done.reshape(shape), 'cls', 0, 1, tiled=True)  11.2 us
    pallas_call x1, Pallas kernels, react_all(): pl.pallas_call(functools.partial(react_kernel, 256), out_shape=jax.ShapeD...  11.1 us
    ppermute x2, starting transfers between devices, passed_along(): return lax.ppermute(x, axis, pairs)  6.17 us
    ppermute x2, waiting for transfers between devices, passed_along(): return lax.ppermute(x, axis, pairs)  3.92 us
    unnamed x8, local copies, waits for them, and re-layouts  2.05 us
    reshape x1, local copies, waits for them, and re-layouts, body(): return lax.all_to_all(done.reshape(shape), 'cls', 0, 1, tiled=True)  1.58 us
    reshape x1, local copies, waits for them, and re-layouts, body(): field = concentration.reshape(group, layers, CX, CY)  1.51 us
  transfers between devices with their start and end apart: 2, of which 1 were waited for; matrix products, arithmetic and copies ran while one was open for 1% of the time, Pallas kernels for 0%

profile of v1, /device:TPU:0, one launch (start us, length us, event | category | flops | bytes accessed | tf_op | source)
XLA Modules:
  0.0 54.3 jit_solution(1743537722087698831)
XLA Ops:
  0.0 0.0 copy-start.1
  0.0 1.5 %reshape.25 = f32[16,4,4,512]{3,2,1,0:T(4,128)S(1)} reshape(f32[16,4,2048]{2,1,0:T(4,128)} %param.8) | data formatting | bytes 1048576 | tf_op jit(solution)/shard_map/reshape | solution.py:130
  1.5 0.0 copy-done.1
  1.5 0.0 copy-start.2
  1.5 0.1 reshape.26
  1.6 0.6 %copy-done.2 = s32[2048]{0:T(1024)S(1)} copy-done((s32[2048]{0:T(1024)S(1)}, s32[2048]{0:T(1024)}, u32[]{:S(2)}) %copy-start.2) | copy-done | bytes 8216
  2.3 0.2 pad_maximum_fusion.6
  2.5 0.2 fusion.15
  2.7 4.9 %collective-permute-start = (f32[19,4,1,512]{3,2,1,0:T(1,128)S(1)}, f32[19,4,1,512]{3,2,1,0:T(1,128)S(1)}, u32[]{:S(2)}, u32[]{:S(2)}) collective-permute-start(f32[19,4,1,512]{3,2,1,0:T(1,128)S(1)} %get-tuple-element.9), channel_id=1, source_target_pairs={{0,4},{4,8},{8,12},{12,16},{16,20},{20,24},{24,28},{1,5},{5,9},{9,... | collective-permute-start | bytes 466952 | tf_op jit(solution)/shard_map/ppermute | solution.py:17
  7.6 1.3 %collective-permute-start.1 = (f32[19,4,1,512]{3,2,1,0:T(1,128)S(1)}, f32[19,4,1,512]{3,2,1,0:T(1,128)S(1)}, u32[]{:S(2)}, u32[]{:S(2)}) collective-permute-start(f32[19,4,1,512]{3,2,1,0:T(1,128)S(1)} %get-tuple-element.10), channel_id=1, source_target_pairs={{4,0},{8,4},{12,8},{16,12},{20,16},{24,20},{28,24},{5,1},{9,5},{13... | collective-permute-start | bytes 466952 | tf_op jit(solution)/shard_map/ppermute | solution.py:17
  8.9 0.1 maximum_bitcast_fusion.1
  9.0 0.0 copy-start.3
  9.0 0.6 %copy-done.3 = f32[16]{0:T(128)S(1)} copy-done((f32[16]{0:T(128)S(1)}, f32[16]{0:T(128)}, u32[]{:S(2)}) %copy-start.3) | copy-done | bytes 88
  9.7 0.1 broadcast_multiply_fusion
  9.8 0.0 copy-start
  9.8 0.8 %copy-done = f32[16,4,4,512]{3,2,1,0:T(4,128)} copy-done((f32[16,4,4,512]{3,2,1,0:T(4,128)}, f32[16,4,4,512]{3,2,1,0:T(4,128)S(1)}, u32[]{:S(2)}) %copy-start) | copy-done | bytes 524312
  10.6 0.4 fusion.4
  11.0 0.0 collective-permute-done
  11.0 3.9 %collective-permute-done.1 = f32[19,4,1,512]{3,2,1,0:T(1,128)S(1)} collective-permute-done((f32[19,4,1,512]{3,2,1,0:T(1,128)S(1)}, f32[19,4,1,512]{3,2,1,0:T(1,128)S(1)}, u32[]{:S(2)}, u32[]{:S(2)}) %collective-permute-start.1) | collective-permute-done | bytes 155680 | tf_op jit(solution)/shard_map/ppermute | solution.py:17
  15.0 0.1 maximum_bitcast_fusion
  15.0 0.0 slice-start
  15.1 0.5 fusion.1
  15.5 0.5 slice-done
  16.0 0.6 %fusion.8 = f32[16,4,4,512]{3,2,1,0:T(4,128)S(1)} fusion(f32[16,4,4,513]{3,2,1,0:T(4,128)S(1)} %fusion.4, f32[16,4,4,512]{3,2,1,0:T(4,128)S(1)} %reshape.25, f32[16,4,5,512]{3,2,1,0:T(8,128)S(1)} %fusion.1, f32[16,3,4,512]{3,2,1,0:T(4,128)S(1)} %slice-done, f32[16]{0:T(128)S(1)} %copy-done.3), kind=kLoop, calls=%fused_computation.22 | loop fusion | flops 917504 | bytes 3539008 | tf_op jit(solution)/shard_map/add | solution.py:148
  16.7 0.4 reshape.30
  17.1 0.3 copy.14
  17.4 11.9 %all_to_all.33 = f32[16,4,2048]{2,0,1:T(8,128)} all-to-all(f32[16,4,2048]{2,0,1:T(8,128)S(1)} %copy.14), channel_id=1, replica_groups=mesh['tile'=8,'cls'=4] {'cls'}, dimensions={1} | all-to-all | bytes 1048576 | tf_op jit(solution)/shard_map/all_to_all | solution.py:150
  29.3 11.1 %shard_map.82 = f32[64,2048]{1,0:T(8,128)} custom-call(s32[64,64]{1,0:T(8,128)} %levels_ref.1, s32[64,64]{1,0:T(8,128)} %target_ref.1, s32[64,64]{1,0:T(8,128)} %weights_ref.1, f32[1,64]{1,0:T(1,128)} %bitcast.24, f32[64,2048]{1,0:T(8,128)} %bitcast.21), custom_call_target="tpu_custom_call" | custom-call | tf_op jit(solution)/shard_map/pallas_call | solution.py:107
  40.4 1.6 %copy.12 = f32[64,1,2048]{2,1,0:T(1,128)S(1)} copy(f32[64,1,2048]{2,0,1:T(8,128)} %bitcast.22) | data formatting | bytes 1048576 | tf_op jit(solution)/shard_map/reshape | solution.py:155
  42.0 11.2 %all_to_all.34 = f32[64,1,2048]{2,1,0:T(1,128)S(1)} all-to-all(f32[64,1,2048]{2,1,0:T(1,128)S(1)} %copy.12), channel_id=1, replica_groups=mesh['tile'=8,'cls'=4] {'cls'}, dimensions={0} | all-to-all | bytes 1048576 | tf_op jit(solution)/shard_map/all_to_all | solution.py:155
  53.2 1.1 %copy.16 = f32[4,16,1,2048]{3,0,1,2:T(4,128)} copy(f32[4,16,1,2048]{3,2,1,0:T(1,128)S(1)} %bitcast.23) | data formatting | bytes 1048576 | tf_op jit(solution)/shard_map/all_to_all | solution.py:155
  (5 shorter events, 0.0 us)
Async XLA Ops:
  0.0 1.5 %copy-start.1 = (f32[2,4,2048]{2,1,0:T(4,128)S(1)}, f32[2,4,2048]{2,1,0:T(4,128)}, u32[]{:S(2)}) copy-start(f32[2,4,2048]{2,1,0:T(4,128)} %param.9) | copy-start | bytes 196612
  1.5 0.7 %copy-start.2 = (s32[2048]{0:T(1024)S(1)}, s32[2048]{0:T(1024)}, u32[]{:S(2)}) copy-start(s32[2048]{0:T(1024)} %param.10) | copy-start | bytes 24580
  2.7 8.3 %collective-permute-start = (f32[19,4,1,512]{3,2,1,0:T(1,128)S(1)}, f32[19,4,1,512]{3,2,1,0:T(1,128)S(1)}, u32[]{:S(2)}, u32[]{:S(2)}) collective-permute-start(f32[19,4,1,512]{3,2,1,0:T(1,128)S(1)} %get-tuple-element.9), channel_id=1, source_target_pairs={{0,4},{4,8},{8,12},{12,16},{16,20},{20,24},{24,28},{1,5},{5,9},{9,... | collective-permute-start | bytes 466952 | tf_op jit(solution)/shard_map/ppermute | solution.py:17
  7.6 7.4 %collective-permute-start.1 = (f32[19,4,1,512]{3,2,1,0:T(1,128)S(1)}, f32[19,4,1,512]{3,2,1,0:T(1,128)S(1)}, u32[]{:S(2)}, u32[]{:S(2)}) collective-permute-start(f32[19,4,1,512]{3,2,1,0:T(1,128)S(1)} %get-tuple-element.10), channel_id=1, source_target_pairs={{4,0},{8,4},{12,8},{16,12},{20,16},{24,20},{28,24},{5,1},{9,5},{13... | collective-permute-start | bytes 466952 | tf_op jit(solution)/shard_map/ppermute | solution.py:17
  9.0 0.7 %copy-start.3 = (f32[16]{0:T(128)S(1)}, f32[16]{0:T(128)}, u32[]{:S(2)}) copy-start(f32[16]{0:T(128)} %param.11) | copy-start | bytes 196
  9.8 0.8 %copy-start = (f32[16,4,4,512]{3,2,1,0:T(4,128)}, f32[16,4,4,512]{3,2,1,0:T(4,128)S(1)}, u32[]{:S(2)}) copy-start(f32[16,4,4,512]{3,2,1,0:T(4,128)S(1)} %broadcast_multiply_fusion) | copy-start | bytes 1572868
  15.0 1.0 %slice-start = ((f32[16,4,4,512]{3,2,1,0:T(4,128)}), f32[16,3,4,512]{3,2,1,0:T(4,128)S(1)}, s32[]{:S(2)}) async-start(f32[16,4,4,512]{3,2,1,0:T(4,128)} %copy-done), calls=%async_computation.2 | async-start | bytes 786432 | tf_op jit(solution)/shard_map/slice | solution.py:148

commit v2 on v1

v2 whole, which is shorter than its diff:
```python
import functools

import jax
import jax.numpy as jnp
from jax import lax
from jax.experimental import pallas as pl
from jax.experimental.pallas import tpu as pltpu
from jax.sharding import PartitionSpec as P

CY = 512
CX = 4
half_scale = 0.5e-05
STEP = 16


def split_pair(value, lane, total):
    high = value.astype(jnp.bfloat16).astype(jnp.float32)
    return jnp.where(lane < total, high, value - high).astype(jnp.bfloat16)


def quad_rows(total):
    return sum(STEP * (total - first) for first in range(0, total, STEP))


def build_tables(levels_ref, target_ref, weights_ref, rate_ref, quad_ref, lin_ref):
    total = levels_ref.shape[0]
    wide = 2 * total
    levels = levels_ref[...].astype(jnp.float32)
    levels = jnp.concatenate([levels, levels], 1)
    target = target_ref[...]
    target = jnp.concatenate([target, target], 1)
    row = lax.broadcasted_iota(jnp.int32, (total, wide), 0)
    lane = lax.broadcasted_iota(jnp.int32, (total, wide), 1)
    col = jnp.where(lane < total, lane, lane - total)
    twice = 2.0 * levels
    birth = jnp.where(col < row, twice, jnp.where(col == row, levels, 0.0))
    offset = 0
    for first in range(0, total, STEP):
        count = total - first
        rank = row[first:]
        for i in range(first, first + STEP):
            value = jnp.where(target[i : i + 1] == rank, birth[i : i + 1], 0.0)
            value = value - jnp.where(rank == i, twice[i : i + 1], 0.0)
            packed = split_pair(value, lane[first:], total)
            quad_ref[offset : offset + count, :wide] = packed
            quad_ref[offset : offset + count, wide:] = packed
            offset += count
    weights = weights_ref[...].astype(jnp.float32)
    weights = jnp.concatenate([weights, weights], 1)
    rate = rate_ref[...]
    rate = jnp.concatenate([rate, rate], 1)
    lower = jnp.where(row <= col, weights, 0.0)
    frag = lower / jnp.sum(lower, axis=0, keepdims=True)
    value = frag * rate - jnp.where(row == col, rate, 0.0)
    packed = split_pair(value, lane, total)
    lin_ref[:, :wide] = packed
    lin_ref[:, wide:] = packed


def react(now, quad_ref, lin_ref):
    total = now.shape[0]
    high = now.astype(jnp.bfloat16)
    low = (now - high.astype(jnp.float32)).astype(jnp.bfloat16)
    stack = jnp.concatenate([high, high, low, low], 0)
    lin = jnp.dot(lin_ref[...], stack, preferred_element_type=jnp.float32)
    gain = None
    offset = 0
    for first in range(0, total, STEP):
        count = total - first
        made = jnp.dot(
            quad_ref[offset : offset + STEP * count, :], stack, preferred_element_type=jnp.float32
        )
        part = made[:count] * now[first : first + 1]
        for r in range(1, STEP):
            part = part + made[r * count : (r + 1) * count] * now[first + r : first + r + 1]
        gain = part if gain is None else jnp.concatenate([gain[:first], gain[first:] + part], 0)
        offset += STEP * count
    return now + gain * half_scale + lin


MESH = pl.DeviceIdType.MESH


def step_kernel(
    tiles,
    peers,
    conc_ref,
    speed_ref,
    water_ref,
    settling_ref,
    rate_ref,
    levels_ref,
    target_ref,
    weights_ref,
    out_ref,
    quad_ref,
    lin_ref,
    moved_ref,
    whole_ref,
    done_ref,
    halo_c,
    halo_u,
    halo_w,
    halo_send,
    halo_recv,
    out_send,
    out_recv,
    back_send,
    back_recv,
):
    layers, group, _ = conc_ref.shape
    own = layers // peers
    tile = lax.axis_index("tile")
    me = lax.axis_index("cls")
    has_west = tile > 0
    has_east = tile < tiles - 1

    barrier = pltpu.get_barrier_semaphore()
    for d in range(1, peers):
        pl.semaphore_signal(
            barrier, inc=1, device_id={"cls": lax.rem(me + d, peers)}, device_id_type=MESH
        )

    @pl.when(has_west)
    def _():
        pl.semaphore_signal(barrier, inc=1, device_id={"tile": tile - 1}, device_id_type=MESH)

    @pl.when(has_east)
    def _():
        pl.semaphore_signal(barrier, inc=1, device_id={"tile": tile + 1}, device_id_type=MESH)

    build_tables(levels_ref, target_ref, weights_ref, rate_ref, quad_ref, lin_ref)

    before = lax.div(tile + tiles - 1, tiles)
    after = lax.div(2 * (tiles - 1) - tile, tiles)
    pl.semaphore_wait(barrier, peers - 1 + before + after)

    def cols(x):
        return pl.ds(pl.multiple_of(x * CY, CY), CY)

    def halo(side):
        at = cols(0 if side == 0 else CX - 1)
        to = 1 - side
        where = tile - 1 if side == 0 else tile + 1
        parts = (
            (speed_ref.at[0, :, at], halo_u.at[to]),
            (water_ref.at[:, at], halo_w.at[to]),
            (conc_ref.at[:, :, at], halo_c.at[to]),
        )
        return [
            pltpu.make_async_remote_copy(
                src_ref=part,
                dst_ref=place,
                send_sem=halo_send.at[side, n],
                recv_sem=halo_recv.at[to, n],
                device_id={"tile": where},
                device_id_type=MESH,
            )
            for n, (part, place) in enumerate(parts)
        ]

    def taken(side):
        at = cols(0)
        parts = (
            (speed_ref.at[0, :, at], halo_u.at[side]),
            (water_ref.at[:, at], halo_w.at[side]),
            (conc_ref.at[:, :, at], halo_c.at[side]),
        )
        where = tile - 1 if side == 0 else tile + 1
        return [
            pltpu.make_async_remote_copy(
                src_ref=part,
                dst_ref=place,
                send_sem=halo_send.at[side, n],
                recv_sem=halo_recv.at[side, n],
                device_id={"tile": where},
                device_id_type=MESH,
            )
            for n, (part, place) in enumerate(parts)
        ]

    for side, there in ((0, has_west), (1, has_east)):

        @pl.when(there)
        def _():
            for copy in halo(side):
                copy.start()

        @pl.when(jnp.logical_not(there))
        def _():
            halo_c[side] = jnp.zeros(halo_c.shape[1:], jnp.float32)
            halo_u[side] = jnp.zeros(halo_u.shape[1:], jnp.float32)
            halo_w[side] = jnp.zeros(halo_w.shape[1:], jnp.int32)

    def forward(d, x, s):
        p = lax.rem(me + d, peers)
        return pltpu.make_async_remote_copy(
            src_ref=moved_ref.at[p * own + s, :, cols(x)],
            dst_ref=whole_ref.at[s, pl.ds(pl.multiple_of(me * group, group), group), cols(x)],
            send_sem=out_send.at[d - 1, x, s],
            recv_sem=out_recv.at[d - 1, x, s],
            device_id={"cls": p},
            device_id_type=MESH,
        )

    def backward(d, x, s):
        p = lax.rem(me + d, peers)
        return pltpu.make_async_remote_copy(
            src_ref=done_ref.at[s, pl.ds(pl.multiple_of(p * group, group), group), cols(x)],
            dst_ref=out_ref.at[me * own + s, :, cols(x)],
            send_sem=back_send.at[d - 1, x, s],
            recv_sem=back_recv.at[d - 1, x, s],
            device_id={"cls": p},
            device_id_type=MESH,
        )

    def row_of(x):
        at = cols(x)
        return speed_ref[0, :, at], water_ref[:, at].astype(jnp.float32)

    def halo_row(side):
        return halo_u[side], halo_w[side].astype(jnp.float32)

    def transport(x):
        at = cols(x)
        u, w = row_of(x)
        u_low, w_low = row_of(x - 1) if x > 0 else halo_row(0)
        u_high, w_high = row_of(x + 1) if x < CX - 1 else halo_row(1)
        face_low = 0.5 * (u_low + u) * (w_low * w)
        face_high = 0.5 * (u + u_high) * (w * w_high)
        v = speed_ref[1, :, at]
        lane = lax.broadcasted_iota(jnp.int32, v.shape, 1)
        w_full = jnp.broadcast_to(w, v.shape)
        side_high = 0.5 * (v + pltpu.roll(v, CY - 1, 1)) * (w_full * pltpu.roll(w_full, CY - 1, 1))
        side_high = jnp.where(lane == CY - 1, 0.0, side_high)
        side_low = pltpu.roll(side_high, 1, 1)
        up = jnp.maximum
        down = jnp.minimum
        centre = (
            1.0 - up(face_high, 0.0) + down(face_low, 0.0) - up(side_high, 0.0) + down(side_low, 0.0)
        )
        west = up(face_low, 0.0)
        east = -down(face_high, 0.0)
        south = up(side_low, 0.0)
        north = -down(side_high, 0.0)
        settle = jnp.broadcast_to(settling_ref[...], (group, CY))
        for l in range(layers):
            c = conc_ref[l, :, at]
            c_west = conc_ref[l, :, cols(x - 1)] if x > 0 else halo_c[0, l]
            c_east = conc_ref[l, :, cols(x + 1)] if x < CX - 1 else halo_c[1, l]
            moved = (
                (centre[l : l + 1] - settle) * c
                + west[l : l + 1] * c_west
                + east[l : l + 1] * c_east
                + south[l : l + 1] * pltpu.roll(c, 1, 1)
                + north[l : l + 1] * pltpu.roll(c, CY - 1, 1)
            )
            if l > 0:
                moved = moved + settle * conc_ref[l - 1, :, at]
            moved_ref[l, :, at] = moved
        for s in range(own):
            whole_ref[s, pl.ds(pl.multiple_of(me * group, group), group), at] = moved_ref[
                me * own + s, :, at
            ]
        for s in range(own):
            for d in range(1, peers):
                forward(d, x, s).start()

    for x in range(1, CX - 1):
        transport(x)
    for side, there, x in ((1, has_east, CX - 1), (0, has_west, 0)):

        @pl.when(there)
        def _():
            for copy in taken(side):
                copy.wait_recv()

        transport(x)

    half = CY // 2

    def react_row(q, carry):
        x = lax.rem(q + 1, CX)
        for s in range(own):
            for d in range(1, peers):
                forward(d, x, s).wait_recv()

            def part(h, carry):
                at = pl.ds(pl.multiple_of(x * CY + h * half, half), half)
                now = react(whole_ref[s, :, at], quad_ref, lin_ref)
                done_ref[s, :, at] = react(now, quad_ref, lin_ref)
                return carry

            lax.fori_loop(0, 2, part, 0)
            out_ref[me * own + s, :, cols(x)] = done_ref[
                s, pl.ds(pl.multiple_of(me * group, group), group), cols(x)
            ]
            for d in range(1, peers):
                backward(d, x, s).start()
        return carry

    lax.fori_loop(0, CX, react_row, 0)

    for side, there in ((0, has_west), (1, has_east)):

        @pl.when(there)
        def _():
            for copy in halo(side):
                copy.wait_send()

    def finish(x, carry):
        for s in range(own):
            for d in range(1, peers):
                forward(d, x, s).wait_send()
                copy = backward(d, x, s)
                copy.wait_send()
                copy.wait_recv()
        return carry

    lax.fori_loop(0, CX, finish, 0)


def body(
    tiles,
    peers,
    concentration,
    velocity,
    land_mask,
    settling,
    breakage_rate,
    kernel_levels,
    pair_target,
    fragment_weights,
):
    group, layers, columns = concentration.shape
    total = kernel_levels.shape[0]
    own = layers // peers
    vmem = pl.BlockSpec(memory_space=pltpu.VMEM)
    dma = pltpu.SemaphoreType.DMA
    done = pl.pallas_call(
        functools.partial(step_kernel, tiles, peers),
        out_shape=jax.ShapeDtypeStruct((layers, group, columns), jnp.float32),
        in_specs=[vmem] * 8,
        out_specs=vmem,
        scratch_shapes=[
            pltpu.VMEM((quad_rows(total), 4 * total), jnp.bfloat16),
            pltpu.VMEM((total, 4 * total), jnp.bfloat16),
            pltpu.VMEM((layers, group, columns), jnp.float32),
            pltpu.VMEM((own, total, columns), jnp.float32),
            pltpu.VMEM((own, total, columns), jnp.float32),
            pltpu.VMEM((2, layers, group, CY), jnp.float32),
            pltpu.VMEM((2, layers, CY), jnp.float32),
            pltpu.VMEM((2, 1, CY), jnp.int32),
            dma((2, 3)),
            dma((2, 3)),
            dma((peers - 1, CX, own)),
            dma((peers - 1, CX, own)),
            dma((peers - 1, CX, own)),
            dma((peers - 1, CX, own)),
        ],
        compiler_params=pltpu.CompilerParams(collective_id=0, has_side_effects=True),
    )(
        jnp.transpose(concentration, (1, 0, 2)),
        velocity,
        land_mask.reshape(1, columns),
        settling.reshape(group, 1),
        breakage_rate.reshape(1, total),
        kernel_levels,
        pair_target,
        fragment_weights,
    )
    return jnp.transpose(done, (1, 0, 2))


def solution(mesh):
    return jax.shard_map(
        functools.partial(body, mesh.shape["tile"], mesh.shape["cls"]),
        mesh=mesh,
        in_specs=(
            P("cls", None, "tile"),
            P(None, None, "tile"),
            P("tile"),
            P("cls"),
            P(),
            P(),
            P(),
            P(),
        ),
        out_specs=P("cls", None, "tile"),
        check_vma=False,
    )
```

time: 54.7 us -> 30.7 us (0.56)
  the two profiles are of different devices: /device:TPU:0 before, /device:TPU:9 now
where the time goes in v2:
time: 30.7 us; the launch traced here: 30.5 us
  Pallas kernels  24.8 us (81%)
  local copies, waits for them, and re-layouts  5.64 us (18%)
    pallas_call x1, Pallas kernels, body(): pl.pallas_call(functools.partial(step_kernel, tiles, peers), out_shape=ja...  24.8 us
    unnamed x3, local copies, waits for them, and re-layouts  2.8 us
    transpose x1, local copies, waits for them, and re-layouts, body(): return jnp.transpose(done, (1, 0, 2))  2.17 us
    reshape x1, local copies, waits for them, and re-layouts, body(): settling.reshape(group, 1)  0.67 us

profile of v2, /device:TPU:9, one launch (start us, length us, event | category | flops | bytes accessed | tf_op | source)
XLA Modules:
  0.0 30.5 jit_solution(5774402999057280328)
XLA Ops:
  0.0 0.0 copy-start
  0.0 0.7 %copy-done = f32[16]{0:T(128)S(1)} copy-done((f32[16]{0:T(128)S(1)}, f32[16]{0:T(128)}, u32[]{:S(2)}) %copy-start) | copy-done | bytes 88
  0.7 0.7 %copy.10.settling_ref = f32[16,1]{1,0:T(8,128)} copy(f32[16,1]{0,1:T(1,128)S(1)} %bitcast.11) | data formatting | bytes 128 | tf_op jit(solution)/shard_map/reshape | solution.py:366
  1.3 2.1 %copy.13 = f32[16,4,2048]{2,0,1:T(8,128)} copy(f32[16,4,2048]{2,1,0:T(4,128)} %param.8) | data formatting | bytes 1048576 | tf_op args[0]
  3.5 24.8 %shard_map.82 = f32[4,16,2048]{2,1,0:T(8,128)} custom-call(f32[4,16,2048]{2,1,0:T(8,128)} %bitcast.8, f32[2,4,2048]{2,1,0:T(4,128)} %speed_ref.1, s32[1,2048]{1,0:T(1,128)} %bitcast.9, f32[16,1]{1,0:T(8,128)} %copy.10.settling_ref, f32[1,64]{1,0:T(1,128)} %bitcast.10, s32[64,64]{1,0:T(8,128)} %levels_ref.1, s32[64,64]{1,0:T(8,128)} %target_ref.1, ...), custom_call_target="tpu_custom_call" | custom-call | tf_op jit(solution)/shard_map/pallas_call | solution.py:340
  28.3 2.2 %copy.11 = f32[16,4,2048]{2,1,0:T(4,128)} copy(f32[16,4,2048]{2,0,1:T(8,128)} %bitcast.7) | data formatting | bytes 1048576 | tf_op jit(solution)/shard_map/transpose | solution.py:372
Async XLA Ops:
  0.0 0.7 %copy-start = (f32[16]{0:T(128)S(1)}, f32[16]{0:T(128)}, u32[]{:S(2)}) copy-start(f32[16]{0:T(128)} %param.11) | copy-start | bytes 196

commit v3 on v2

--- a/solution.py
+++ b/solution.py
@@ -11,6 +11,7 @@
 CX = 4
 half_scale = 0.5e-05
 STEP = 16
+LANES = 128
 
 
 def split_pair(value, lane, total):
@@ -84,7 +85,7 @@
 def step_kernel(
     tiles,
     peers,
-    conc_ref,
+    flat_ref,
     speed_ref,
     water_ref,
     settling_ref,
@@ -95,9 +96,11 @@
     out_ref,
     quad_ref,
     lin_ref,
+    conc_ref,
     moved_ref,
     whole_ref,
     done_ref,
+    back_ref,
     halo_c,
     halo_u,
     halo_w,
@@ -108,7 +111,8 @@
     back_send,
     back_recv,
 ):
-    layers, group, _ = conc_ref.shape
+    layers, group, columns = conc_ref.shape
+    tile_lanes = columns // LANES
     own = layers // peers
     tile = lax.axis_index("tile")
     me = lax.axis_index("cls")
@@ -129,6 +133,12 @@
     def _():
         pl.semaphore_signal(barrier, inc=1, device_id={"tile": tile + 1}, device_id_type=MESH)
 
+    def packed(l, j):
+        return pl.ds(j * layers + l, group, stride=tile_lanes * layers)
+
+    for l in range(layers):
+        for j in range(tile_lanes):
+            conc_ref[l, :, j * LANES : (j + 1) * LANES] = flat_ref[packed(l, j), :]
     build_tables(levels_ref, target_ref, weights_ref, rate_ref, quad_ref, lin_ref)
 
     before = lax.div(tile + tiles - 1, tiles)
@@ -207,7 +217,7 @@
         p = lax.rem(me + d, peers)
         return pltpu.make_async_remote_copy(
             src_ref=done_ref.at[s, pl.ds(pl.multiple_of(p * group, group), group), cols(x)],
-            dst_ref=out_ref.at[me * own + s, :, cols(x)],
+            dst_ref=back_ref.at[me * own + s, :, cols(x)],
             send_sem=back_send.at[d - 1, x, s],
             recv_sem=back_recv.at[d - 1, x, s],
             device_id={"cls": p},
@@ -220,6 +230,13 @@
 
     def halo_row(side):
         return halo_u[side], halo_w[side].astype(jnp.float32)
+
+    square = (group, group)
+    diagonal = lax.broadcasted_iota(jnp.int32, square, 0) == lax.broadcasted_iota(
+        jnp.int32, square, 1
+    )
+    settle = jnp.sum(jnp.where(diagonal, settling_ref[...], 0.0), axis=1, keepdims=True)
+    settle = jnp.broadcast_to(settle, (group, CY))
 
     def transport(x):
         at = cols(x)
@@ -243,7 +260,6 @@
         east = -down(face_high, 0.0)
         south = up(side_low, 0.0)
         north = -down(side_high, 0.0)
-        settle = jnp.broadcast_to(settling_ref[...], (group, CY))
         for l in range(layers):
             c = conc_ref[l, :, at]
             c_west = conc_ref[l, :, cols(x - 1)] if x > 0 else halo_c[0, l]
@@ -292,7 +308,7 @@
                 return carry
 
             lax.fori_loop(0, 2, part, 0)
-            out_ref[me * own + s, :, cols(x)] = done_ref[
+            back_ref[me * own + s, :, cols(x)] = done_ref[
                 s, pl.ds(pl.multiple_of(me * group, group), group), cols(x)
             ]
             for d in range(1, peers):
@@ -308,16 +324,16 @@
             for copy in halo(side):
                 copy.wait_send()
 
-    def finish(x, carry):
+    for x in [*range(1, CX), 0]:
         for s in range(own):
             for d in range(1, peers):
                 forward(d, x, s).wait_send()
                 copy = backward(d, x, s)
                 copy.wait_send()
                 copy.wait_recv()
-        return carry
-
-    lax.fori_loop(0, CX, finish, 0)
+        for l in range(layers):
+            for j in range(x * CY // LANES, (x + 1) * CY // LANES):
+                out_ref[packed(l, j), :] = back_ref[l, :, j * LANES : (j + 1) * LANES]
 
 
 def body(
@@ -335,19 +351,23 @@
     group, layers, columns = concentration.shape
     total = kernel_levels.shape[0]
     own = layers // peers
+    flat = concentration.reshape(group, layers, columns // LANES, LANES)
+    flat = jnp.transpose(flat, (0, 2, 1, 3)).reshape(-1, LANES)
     vmem = pl.BlockSpec(memory_space=pltpu.VMEM)
     dma = pltpu.SemaphoreType.DMA
     done = pl.pallas_call(
         functools.partial(step_kernel, tiles, peers),
-        out_shape=jax.ShapeDtypeStruct((layers, group, columns), jnp.float32),
+        out_shape=jax.ShapeDtypeStruct((group * layers * columns // LANES, LANES), jnp.float32),
         in_specs=[vmem] * 8,
         out_specs=vmem,
         scratch_shapes=[
             pltpu.VMEM((quad_rows(total), 4 * total), jnp.bfloat16),
             pltpu.VMEM((total, 4 * total), jnp.bfloat16),
             pltpu.VMEM((layers, group, columns), jnp.float32),
+            pltpu.VMEM((layers, group, columns), jnp.float32),
             pltpu.VMEM((own, total, columns), jnp.float32),
             pltpu.VMEM((own, total, columns), jnp.float32),
+            pltpu.VMEM((layers, group, columns), jnp.float32),
             pltpu.VMEM((2, layers, group, CY), jnp.float32),
             pltpu.VMEM((2, layers, CY), jnp.float32),
             pltpu.VMEM((2, 1, CY), jnp.int32),
@@ -360,16 +380,17 @@
         ],
         compiler_params=pltpu.CompilerParams(collective_id=0, has_side_effects=True),
     )(
-        jnp.transpose(concentration, (1, 0, 2)),
+        flat,
         velocity,
         land_mask.reshape(1, columns),
-        settling.reshape(group, 1),
+        settling.reshape(1, group),
         breakage_rate.reshape(1, total),
         kernel_levels,
         pair_target,
         fragment_weights,
     )
-    return jnp.transpose(done, (1, 0, 2))
+    done = done.reshape(group, columns // LANES, layers, LANES)
+    return jnp.transpose(done, (0, 2, 1, 3)).reshape(group, layers, columns)
 
 
 def solution(mesh):

time: 30.7 us -> 27 us (0.88)
  local copies, waits for them, and re-layouts: 5.64 us -> 1.89 us
    transpose x1 -> x0, local copies, waits for them, and re-layouts: 2.17 us -> none  [body(): return jnp.transpose(done, (1, 0, 2))]
    unnamed x3 -> x1, local copies, waits for them, and re-layouts: 2.8 us -> 1.89 us
    reshape x1 -> x0, local copies, waits for them, and re-layouts: 0.67 us -> none  [body(): settling.reshape(group, 1)]
where the time goes in v3:
time: 27 us; the launch traced here: 26.8 us
  Pallas kernels  24.9 us (92%)
  local copies, waits for them, and re-layouts  1.89 us (7%)
    pallas_call x1, Pallas kernels, body(): pl.pallas_call(functools.partial(step_kernel, tiles, peers), out_shape=ja...  24.9 us
    unnamed x1, local copies, waits for them, and re-layouts  1.89 us

profile of v3, /device:TPU:9, one launch (start us, length us, event | category | flops | bytes accessed | tf_op | source)
XLA Modules:
  0.0 26.8 jit_solution(10978014887721549002)
XLA Ops:
  0.0 24.9 %shard_map.82 = f32[1024,128]{1,0:T(8,128)} custom-call(f32[1024,128]{1,0:T(8,128)} %bitcast.14, f32[2,4,2048]{2,1,0:T(4,128)} %speed_ref.1, s32[1,2048]{1,0:T(1,128)} %bitcast.15, f32[1,16]{1,0:T(1,128)} %bitcast.16, f32[1,64]{1,0:T(1,128)} %bitcast.17, s32[64,64]{1,0:T(8,128)} %levels_ref.1, s32[64,64]{1,0:T(8,128)} %target_ref.1, s32[64,64]{1,0:T(8,128)} %weights_ref.1), custom_call_target="tpu_custom_call" | custom-call | tf_op jit(solution)/shard_map/pallas_call | solution.py:358
  24.9 1.9 %copy.12 = f32[16,4,2048]{2,1,0:T(4,128)} copy(f32[16,4,2048]{2,1,0:T(4,128)} %bitcast.13) | data formatting | bytes 1048576

commit v4 on v3

--- a/solution.py
+++ b/solution.py
@@ -10,7 +10,7 @@
 CY = 512
 CX = 4
 half_scale = 0.5e-05
-STEP = 16
+STEP = 8
 LANES = 128
 
 
@@ -293,7 +293,7 @@
 
         transport(x)
 
-    half = CY // 2
+    half = CY
 
     def react_row(q, carry):
         x = lax.rem(q + 1, CX)
@@ -307,7 +307,7 @@
                 done_ref[s, :, at] = react(now, quad_ref, lin_ref)
                 return carry
 
-            lax.fori_loop(0, 2, part, 0)
+            part(0, 0)
             back_ref[me * own + s, :, cols(x)] = done_ref[
                 s, pl.ds(pl.multiple_of(me * group, group), group), cols(x)
             ]
@@ -357,7 +357,7 @@
     dma = pltpu.SemaphoreType.DMA
     done = pl.pallas_call(
         functools.partial(step_kernel, tiles, peers),
-        out_shape=jax.ShapeDtypeStruct((group * layers * columns // LANES, LANES), jnp.float32),
+        out_shape=pltpu.VMEM((group * layers * columns // LANES, LANES), jnp.float32),
         in_specs=[vmem] * 8,
         out_specs=vmem,
         scratch_shapes=[
@@ -378,7 +378,7 @@
             dma((peers - 1, CX, own)),
             dma((peers - 1, CX, own)),
         ],
-        compiler_params=pltpu.CompilerParams(collective_id=0, has_side_effects=True),
+        compiler_params=pltpu.CompilerParams(collective_id=0, has_side_effects=True, vmem_limit_bytes=32 * 1024 * 1024),
     )(
         flat,
         velocity,

time: 27 us -> 27.9 us (1.033)
  local copies, waits for them, and re-layouts: 1.89 us -> 6.31 us
  Pallas kernels: 24.9 us -> 21.1 us
    unnamed x1 -> x17, local copies, waits for them, and re-layouts: 1.89 us -> 6.31 us
    pallas_call x1, Pallas kernels: 24.9 us -> 21.1 us  [body(): pl.pallas_call(functools.partial(step_kernel, tiles, peers), out_shape=pl...]
where the time goes in v4:
time: 27.9 us; the launch traced here: 27.5 us
  Pallas kernels  21.1 us (76%)
  local copies, waits for them, and re-layouts  6.31 us (23%)
    pallas_call x1, Pallas kernels, body(): pl.pallas_call(functools.partial(step_kernel, tiles, peers), out_shape=pl...  21.1 us
    unnamed x17, local copies, waits for them, and re-layouts  6.31 us

profile of v4, /device:TPU:9, one launch (start us, length us, event | category | flops | bytes accessed | tf_op | source)
XLA Modules:
  0.0 27.5 jit_solution(7686442782631339269)
XLA Ops:
  0.0 0.0 copy-start.6
  0.0 0.0 copy-start.7
  0.0 0.7 %copy-done.6 = f32[16]{0:T(128)S(1)} copy-done((f32[16]{0:T(128)S(1)}, f32[16]{0:T(128)}, u32[]{:S(2)}) %copy-start.6) | copy-done | bytes 88
  0.7 0.0 copy-done.7
  0.7 0.0 copy-start
  0.7 1.0 %copy-done = f32[16,4,2048]{2,1,0:T(4,128)S(1)} copy-done((f32[16,4,2048]{2,1,0:T(4,128)S(1)}, f32[16,4,2048]{2,1,0:T(4,128)}, u32[]{:S(2)}) %copy-start) | copy-done | bytes 524312
  1.7 0.0 copy-start.1
  1.7 0.8 %copy-done.1 = f32[2,4,2048]{2,1,0:T(4,128)S(1)} copy-done((f32[2,4,2048]{2,1,0:T(4,128)S(1)}, f32[2,4,2048]{2,1,0:T(4,128)}, u32[]{:S(2)}) %copy-start.1) | copy-done | bytes 65560
  2.6 0.0 copy-start.2
  2.6 0.8 %copy-done.2 = s32[64,64]{1,0:T(8,128)S(1)} copy-done((s32[64,64]{1,0:T(8,128)S(1)}, s32[64,64]{1,0:T(8,128)}, u32[]{:S(2)}) %copy-start.2) | copy-done | bytes 16408
  3.3 0.0 copy-start.3
  3.3 0.8 %copy-done.3 = s32[64,64]{1,0:T(8,128)S(1)} copy-done((s32[64,64]{1,0:T(8,128)S(1)}, s32[64,64]{1,0:T(8,128)}, u32[]{:S(2)}) %copy-start.3) | copy-done | bytes 16408
  4.1 0.0 copy-start.4
  4.1 0.8 %copy-done.4 = s32[64,64]{1,0:T(8,128)S(1)} copy-done((s32[64,64]{1,0:T(8,128)S(1)}, s32[64,64]{1,0:T(8,128)}, u32[]{:S(2)}) %copy-start.4) | copy-done | bytes 16408
  4.8 0.0 copy-start.5
  4.8 0.7 %copy-done.5 = s32[2048]{0:T(1024)S(1)} copy-done((s32[2048]{0:T(1024)S(1)}, s32[2048]{0:T(1024)}, u32[]{:S(2)}) %copy-start.5) | copy-done | bytes 8216
  5.5 21.1 %shard_map.82 = f32[1024,128]{1,0:T(8,128)S(1)} custom-call(f32[1024,128]{1,0:T(8,128)S(1)} %bitcast.14, f32[2,4,2048]{2,1,0:T(4,128)S(1)} %copy-done.1, s32[1,2048]{1,0:T(1,128)S(1)} %bitcast.15, f32[1,16]{1,0:T(1,128)S(1)} %bitcast.16, f32[1,64]{1,0:T(1,128)S(1)} %bitcast.17, s32[64,64]{1,0:T(8,128)S(1)} %copy-done.2, s32[64,64]{1,0:T(8,128)S(1)} %copy-done.3, ...), custom_call_target="tpu_custom_call" | custom-call | tf_op jit(solution)/shard_map/pallas_call | solution.py:358
  26.7 0.8 %copy.12 = f32[16,4,2048]{2,1,0:T(4,128)} copy(f32[16,4,2048]{2,1,0:T(4,128)S(1)} %bitcast.13) | data formatting | bytes 1048576
Async XLA Ops:
  0.0 0.7 %copy-start.6 = (f32[16]{0:T(128)S(1)}, f32[16]{0:T(128)}, u32[]{:S(2)}) copy-start(f32[16]{0:T(128)} %param.11) | copy-start | bytes 196
  0.0 0.7 %copy-start.7 = (f32[64]{0:T(128)S(1)}, f32[64]{0:T(128)}, u32[]{:S(2)}) copy-start(f32[64]{0:T(128)} %param.12) | copy-start | bytes 772
  0.7 1.0 %copy-start = (f32[16,4,2048]{2,1,0:T(4,128)S(1)}, f32[16,4,2048]{2,1,0:T(4,128)}, u32[]{:S(2)}) copy-start(f32[16,4,2048]{2,1,0:T(4,128)} %param.8) | copy-start | bytes 1572868
  1.7 0.8 %copy-start.1 = (f32[2,4,2048]{2,1,0:T(4,128)S(1)}, f32[2,4,2048]{2,1,0:T(4,128)}, u32[]{:S(2)}) copy-start(f32[2,4,2048]{2,1,0:T(4,128)} %speed_ref.1) | copy-start | bytes 196612
  2.6 0.8 %copy-start.2 = (s32[64,64]{1,0:T(8,128)S(1)}, s32[64,64]{1,0:T(8,128)}, u32[]{:S(2)}) copy-start(s32[64,64]{1,0:T(8,128)} %levels_ref.1) | copy-start | bytes 49156
  3.3 0.8 %copy-start.3 = (s32[64,64]{1,0:T(8,128)S(1)}, s32[64,64]{1,0:T(8,128)}, u32[]{:S(2)}) copy-start(s32[64,64]{1,0:T(8,128)} %target_ref.1) | copy-start | bytes 49156
  4.1 0.8 %copy-start.4 = (s32[64,64]{1,0:T(8,128)S(1)}, s32[64,64]{1,0:T(8,128)}, u32[]{:S(2)}) copy-start(s32[64,64]{1,0:T(8,128)} %weights_ref.1) | copy-start | bytes 49156
  4.8 0.7 %copy-start.5 = (s32[2048]{0:T(1024)S(1)}, s32[2048]{0:T(1024)}, u32[]{:S(2)}) copy-start(s32[2048]{0:T(1024)} %param.10) | copy-start | bytes 24580

commit v5 on v4

--- a/solution.py
+++ b/solution.py
@@ -378,7 +378,7 @@
             dma((peers - 1, CX, own)),
             dma((peers - 1, CX, own)),
         ],
-        compiler_params=pltpu.CompilerParams(collective_id=0, has_side_effects=True, vmem_limit_bytes=32 * 1024 * 1024),
+        compiler_params=pltpu.CompilerParams(collective_id=0, has_side_effects=True),
     )(
         flat,
         velocity,

time: 27.9 us -> 23.2 us (0.83); the launches traced: 27.5 us -> 23.1 us
  local copies, waits for them, and re-layouts: 6.31 us -> 0.8 us
  Pallas kernels: 21.1 us -> 22.3 us
    unnamed x17 -> x1, local copies, waits for them, and re-layouts: 6.31 us -> 0.8 us
    pallas_call x1, Pallas kernels: 21.1 us -> 22.3 us  [body(): pl.pallas_call(functools.partial(step_kernel, tiles, peers), out_shape=pl...]
where the time goes in v5:
time: 23.2 us; the launch traced here: 23.1 us
  Pallas kernels  22.3 us (96%)
  local copies, waits for them, and re-layouts  0.8 us (3%)
    pallas_call x1, Pallas kernels, body(): pl.pallas_call(functools.partial(step_kernel, tiles, peers), out_shape=pl...  22.3 us
    unnamed x1, local copies, waits for them, and re-layouts  0.8 us

profile of v5, /device:TPU:9, one launch (start us, length us, event | category | flops | bytes accessed | tf_op | source)
XLA Modules:
  0.0 23.1 jit_solution(2225816587400864560)
XLA Ops:
  0.0 22.3 %shard_map.82 = f32[1024,128]{1,0:T(8,128)S(1)} custom-call(f32[1024,128]{1,0:T(8,128)} %bitcast.14, f32[2,4,2048]{2,1,0:T(4,128)} %speed_ref.1, s32[1,2048]{1,0:T(1,128)} %bitcast.15, f32[1,16]{1,0:T(1,128)} %bitcast.16, f32[1,64]{1,0:T(1,128)} %bitcast.17, s32[64,64]{1,0:T(8,128)} %levels_ref.1, s32[64,64]{1,0:T(8,128)} %target_ref.1, s32[64,64]{1,0:T(8,128)} %weights_ref.1), custom_call_target="tpu_custom_call" | custom-call | tf_op jit(solution)/shard_map/pallas_call | solution.py:358
  22.3 0.8 %copy.12 = f32[16,4,2048]{2,1,0:T(4,128)} copy(f32[16,4,2048]{2,1,0:T(4,128)S(1)} %bitcast.13) | data formatting | bytes 1048576
